TPU v7x, 32 devices: a whole 2x2x4 slice. The times are simulated.
32 devices in a mesh: dp: 8 (over z, x), seq: 4 (over y, core).
Axes of the slice: x: 2, y: 2, z: 4, core: 2. Of those that a mesh axis runs over, the one named last changes fastest.
Arguments:
- tokens: bfloat16 [4608, 3584], P('dp'), may hold values from -6 to 6
- positions: int32 [3, 4608], P(None, 'dp'), may hold values from 0 to 2047
- loss_mask: int32 [4608], P('dp'), may hold values from 0 to 1, as said below
- sample_tokens: int32 [8, 3], replicated, may hold values from 96 to 384, as said below
- dest_slot: int32 [4608], P('dp'), may hold values from 0 to 6143, as said below
- norm_gain: float32 [3584], replicated, may hold values from 0.5 to 1.5
- q_weight: bfloat16 [3584, 2048], P(None, 'seq'), may hold values from -0.09375 to 0.09375
- k_weight: bfloat16 [3584, 512], P(None, 'seq'), may hold values from -0.09375 to 0.09375
- v_weight: bfloat16 [3584, 512], P(None, 'seq'), may hold values from -0.09375 to 0.09375
- q_bias: float32 [2048], P('seq'), may hold values from -3 to 3
- k_bias: float32 [512], P('seq'), may hold values from -3 to 3
- v_bias: float32 [512], P('seq'), may hold values from -3 to 3
- o_weight: bfloat16 [2048, 3584], P('seq'), may hold values from -0.125 to 0.125
Outputs:
- mixed: bfloat16 [6144, 3584], P(('dp', 'seq'))
- token_weight: float32 [6144], P(('dp', 'seq'))
Inputs may be any that keep to these rules, and one draw needn't show every extreme that they name: `sample_tokens`: row r gives the token counts of the samples in the buckets of receiver r, of 384, 192 and 192 slots; each count lies between half of its bucket's slots and all of them. Some receiver has all three buckets full. All counts together equal the number of rows of tokens. `dest_slot`: every row has a slot of its own, and the slots that rows take are exactly the first sample_tokens[r, b] slots of each bucket b of each receiver r. Of the rows of one sender at most 96 go to one receiver; a receiver whose buckets are all full takes exactly 96 rows from every sender. `loss_mask`: the first of each sender's 576 rows is 1.
All inputs are finite; a program needn't handle non-finite values.
Results may differ from a plain program's by a relative error of at most 0.015.
Values may be sent and summed in bfloat16 or wider, within the bound.
A program may use at most 128 MiB of HBM per device.

v0:
```python
import functools
import math

import jax
import jax.numpy as jnp
from jax import lax
from jax.experimental import pallas as pl
from jax.experimental.pallas import tpu as pltpu
from jax.sharding import PartitionSpec as P

DH = 128
BUCKET = 384
LANES = 128

NORM_EPSILON = 1e-06
ROPE_BASE = 1000000.0
F32 = jnp.float32
BF16 = jnp.bfloat16


def iota(shape, axis):
    return lax.broadcasted_iota(jnp.int32, shape, axis)


def rotary_tables(pos_ref, cos_out, sin_out):
    ids = pos_ref[...]
    rows = ids.shape[1]
    high = ids // 32
    low = ids - high * 32
    kind = iota((8, rows), 0)
    split = jnp.zeros((8, rows), jnp.int32)
    for axis in range(3):
        split = jnp.where(kind == 2 * axis, high[axis : axis + 1], split)
        split = jnp.where(kind == 2 * axis + 1, low[axis : axis + 1], split)
    half_size = DH // 2
    lane, row = iota((8, DH), 1), iota((8, DH), 0)
    pair = lane % half_size
    time_limit = DH // 8
    height_limit = time_limit + 3 * DH // 16
    axis = jnp.where(pair < time_limit, 0, jnp.where(pair < height_limit, 1, 2))
    pick = jnp.where(row == 2 * axis, 32.0, jnp.where(row == 2 * axis + 1, 1.0, 0.0))
    chosen = lax.dot_general(
        split.astype(F32).astype(BF16), pick.astype(BF16), (((0,), (0,)), ((), ())),
        preferred_element_type=F32,
    )
    turn_at = iota((1, DH), 1)
    power = (turn_at % half_size).astype(F32)
    angles = chosen * jnp.exp(power * (-2.0 * math.log(ROPE_BASE) / DH))
    cos_out[...] = jnp.cos(angles)
    sin_out[...] = jnp.sin(angles) * jnp.where(turn_at < half_size, -1.0, 1.0)


def pack_plan(peers, slot_count, group, slot_ref, mask_ref, select_out, info_out):
    rows = slot_ref.shape[0]
    slots = slot_ref[...][None, :]
    peer = slots // slot_count
    local = slots - peer * slot_count + 1
    mask = mask_ref[...][None, :].astype(F32)
    mask_sum = jnp.sum(mask, axis=1, keepdims=True)
    hot = jnp.where(iota((peers, rows), 0) == peer, 1.0, 0.0)
    earlier = jnp.where(iota((rows, rows), 0) < iota((rows, rows), 1), 1.0, 0.0).astype(BF16)
    counts = jnp.dot(hot.astype(BF16), earlier, preferred_element_type=F32)
    rank = jnp.sum(hot * counts, axis=0, keepdims=True).astype(jnp.int32)
    place = peer * LANES + rank
    high = local // 32
    kind = iota((8, rows), 0)
    facts = jnp.where(
        kind == 0,
        high.astype(F32),
        jnp.where(kind == 1, (local - high * 32).astype(F32), jnp.where(kind == 2, mask, 0.0)),
    ).astype(BF16)
    span = group * LANES
    for g in range(peers // group):
        select = jnp.where(iota((span, rows), 0) + g * span == place, 1.0, 0.0).astype(BF16)
        select_out[g * span : (g + 1) * span, :] = select
        told = lax.dot_general(facts, select, (((1,), (1,)), ((), ())), preferred_element_type=F32)
        told = jnp.where(iota(told.shape, 0) == 3, mask_sum, told)
        for p in range(group):
            info_out[g * group + p] = told[:, p * LANES : (p + 1) * LANES]


def attend(q_slots, kv_slots, lengths, heads, per_kv, kv_count, ctx):
    start = 0
    scale = 1.0 / math.sqrt(DH)
    for size, length in zip((BUCKET, BUCKET // 2, BUCKET // 2), lengths):
        rows = slice(start, start + size)
        q_at, k_at = iota((size, size), 0), iota((size, size), 1)
        allowed = (q_at >= k_at) & (k_at < length)
        live = iota((size, DH), 0) < length
        for h in heads:
            pair = h // per_kv
            key = kv_slots[rows, pair * DH : (pair + 1) * DH]
            value = kv_slots[rows, (kv_count + pair) * DH : (kv_count + pair + 1) * DH]
            cols = slice(h * DH, (h + 1) * DH)
            scores = lax.dot_general(
                q_slots[rows, cols], key, (((1,), (1,)), ((), ())), preferred_element_type=F32
            )
            scores = jnp.where(allowed, scores * scale, -1e30)
            top = jnp.max(scores, axis=1, keepdims=True)
            weights = jnp.exp(scores - top)
            total = jnp.sum(weights, axis=1, keepdims=True)
            out = jnp.dot(weights.astype(BF16), value, preferred_element_type=F32) / total
            ctx[rows, cols] = jnp.where(live, out, 0.0).astype(BF16)
        start += size


def layer_kernel(
    peers, group, seq_count, q_heads, kv_heads, chunk, room, strips,
    tok_hbm, gain_ref, qw_hbm, kw_hbm, vw_hbm, qb_ref, kb_ref, vb_ref, pos_ref,
    slot_ref, mask_ref, ow_hbm,
    mixed_ref, weight_ref,
    x, squares, qw, kvw, ow, pick, told_out, got_info, q_out, q_got, kv_out, kv_got,
    select, padded, q_slots, kv_slots, ctx, own,
    near_out, near_in, mine_out, mine_in, far_out, far_in, cos_ref, sin_ref, wide, ctx_all,
    data_send, data_recv, info_send, info_recv, near_send, near_recv,
    mine_send, mine_recv, far_send, far_recv, load_sem, wide_load_sem,
    wide_send, wide_recv, ctx_send, ctx_recv,
):
    me = lax.axis_index("dp")
    seat = lax.axis_index("seq")
    half = seat // 2
    core = seat % 2
    partner = half * 2 + (1 - core)
    across = (1 - half) * 2 + core
    q_stages = q_out.shape[0]
    per_stage = q_heads // q_stages
    rows, depth = x.shape
    slot_count = q_slots.shape[0]
    part = slot_count // seq_count
    wides = wide.shape[1]
    chunks = ow.shape[1] // chunk
    diagonal = (1 - half) * 2 + (1 - core)
    strip = rows // strips
    kv_cols = kv_heads * DH

    barrier = pltpu.get_barrier_semaphore()
    for d in range(1, peers):
        pl.semaphore_signal(barrier, inc=1, device_id={"dp": (me + d) % peers})
    pl.semaphore_signal(barrier, inc=1, device_id={"seq": partner})
    pl.semaphore_signal(barrier, inc=1, device_id={"seq": across})
    pl.semaphore_signal(barrier, inc=1, device_id={"seq": diagonal})
    token_loads = [
        pltpu.make_async_copy(
            tok_hbm.at[i * strip : (i + 1) * strip], x.at[i * strip : (i + 1) * strip],
            load_sem.at[i],
        )
        for i in range(strips)
    ]
    k_load = pltpu.make_async_copy(kw_hbm, kvw.at[:, :kv_cols], load_sem.at[strips])
    v_load = pltpu.make_async_copy(vw_hbm, kvw.at[:, kv_cols:], load_sem.at[strips + 1])
    q_load = pltpu.make_async_copy(qw_hbm, qw, load_sem.at[strips + 2])
    o_load = pltpu.make_async_copy(ow_hbm.at[:, wides * chunk :], ow, load_sem.at[strips + 3])
    wide_loads = [
        pltpu.make_async_copy(
            ow_hbm.at[:, i * chunk : (i + 1) * chunk], wide.at[seat, i], wide_load_sem.at[i]
        )
        for i in range(wides)
    ]
    for copy in token_loads + [k_load, v_load] + wide_loads + [q_load, o_load]:
        copy.start()

    pack_plan(peers, slot_count, group, slot_ref, mask_ref, pick, told_out)
    rotary_tables(pos_ref, cos_ref, sin_ref)
    gain = gain_ref[...][None, :]
    for i in range(strips):
        token_loads[i].wait()
        at = slice(i * strip, (i + 1) * strip)
        total = jnp.zeros((strip, LANES), F32)
        for c in range(depth // LANES):
            cols = slice(c * LANES, (c + 1) * LANES)
            entry = x[at, cols].astype(F32)
            total = total + entry * entry
            x[at, cols] = (entry * gain[:, cols]).astype(BF16)
        squares[at, :] = jnp.sum(total, axis=1, keepdims=True)
    inverse = lax.rsqrt(squares[...] * (1.0 / depth) + NORM_EPSILON)

    def info_copy(d):
        to = (me + d) % peers
        return pltpu.make_async_remote_copy(
            told_out.at[to], got_info.at[me], info_send.at[d], info_recv.at[d],
            device_id={"dp": to},
        )

    def wide_copy(kind, i):
        index = across if kind == 2 else seat
        return pltpu.make_async_remote_copy(
            wide.at[index, i], wide.at[index, i], wide_send.at[kind, i], wide_recv.at[kind, i],
            device_id={"seq": across if kind == 1 else partner},
        )

    def pass_on(i):
        wide_copy(1, i).wait()
        wide_copy(2, i).start()

    def ctx_copy(stage, kind):
        to = (partner, across, diagonal)[kind]
        cols = slice(stage * per_stage * DH, (stage + 1) * per_stage * DH)
        return pltpu.make_async_remote_copy(
            ctx.at[pl.ds(pl.multiple_of(to * part, part), part), cols],
            ctx_all.at[seat, :, cols], ctx_send.at[stage, kind], ctx_recv.at[stage, kind],
            device_id={"seq": to},
        )

    def data_copy(stage, d):
        to = (me + d) % peers
        source, target = (kv_out, kv_got) if stage == 0 else (q_out, q_got)
        if stage > 0:
            source, target = source.at[stage - 1], target.at[stage - 1]
        return pltpu.make_async_remote_copy(
            source.at[to], target.at[me], data_send.at[stage, d], data_recv.at[stage, d],
            device_id={"dp": to},
        )

    def turn(wide):
        return wide * cos_ref[...] + pltpu.roll(wide, DH // 2, 1) * sin_ref[...]

    def pack(stage, values):
        span = group * LANES
        target, kept = (kv_out, kv_got) if stage == 0 else (q_out, q_got)
        if stage > 0:
            target, kept = target.at[stage - 1], kept.at[stage - 1]
        for g in range(peers // group):
            moved = jnp.dot(
                pick[g * span : (g + 1) * span, :], values, preferred_element_type=F32
            ).astype(BF16)
            for p in range(group):
                target[g * group + p] = moved[p * LANES : p * LANES + room]
        for d in range(1, peers):
            data_copy(stage, d).start()
        kept[me] = target[me]

    pl.semaphore_wait(barrier, peers + 2)
    for d in range(1, peers):
        info_copy(d).start()
    got_info[me] = told_out[me]
    for i in range(wides):
        wide_loads[i].wait()
        wide_copy(1, i).start()
        wide_copy(0, i).start()
    k_load.wait()
    v_load.wait()
    product = jnp.dot(x[...], kvw[...], preferred_element_type=F32)
    pieces = []
    for h in range(2 * kv_heads):
        bias_ref, at = (kb_ref, h) if h < kv_heads else (vb_ref, h - kv_heads)
        bias = bias_ref[at * DH : (at + 1) * DH][None, :]
        head = (product[:, h * DH : (h + 1) * DH] * inverse + bias).astype(BF16)
        if h < kv_heads:
            head = turn(head.astype(F32)).astype(BF16)
        pieces.append(head)
    pack(0, jnp.concatenate(pieces, axis=1))
    q_load.wait()
    for stage in range(q_stages):
        cols = slice(stage * per_stage * DH, (stage + 1) * per_stage * DH)
        product = jnp.dot(x[...], qw[:, cols], preferred_element_type=F32)
        pieces = []
        for i in range(per_stage):
            h = stage * per_stage + i
            bias = qb_ref[h * DH : (h + 1) * DH][None, :]
            head = (product[:, i * DH : (i + 1) * DH] * inverse + bias).astype(BF16)
            pieces.append(turn(head.astype(F32)).astype(BF16))
        pack(stage + 1, jnp.concatenate(pieces, axis=1))

    padded[...] = jnp.zeros_like(padded)
    for d in range(1, peers):
        info_copy(d).wait()
    count = jnp.zeros((1, LANES), F32)
    slot_at = iota((slot_count, LANES), 0).astype(F32)
    facts = []
    filled = [jnp.zeros((1, LANES), F32) for _ in range(3)]
    starts = (0, BUCKET, BUCKET + BUCKET // 2, 2 * BUCKET)
    for p in range(peers):
        told = got_info[p]
        facts.append(told)
        count = count + told[3:4]
        local = told[0:1] * 32.0 + told[1:2] - 1.0
        for b in range(3):
            inside = (local >= float(starts[b])) & (local < float(starts[b + 1]))
            filled[b] = filled[b] + jnp.where(inside, 1.0, 0.0)
        select[:, p * LANES : (p + 1) * LANES] = jnp.where(slot_at == local, 1.0, 0.0).astype(BF16)
    flags = jnp.concatenate(facts, axis=1).astype(BF16)
    own_select = select[pl.ds(pl.multiple_of(seat * part, part), part), :]
    seen = lax.dot_general(flags, own_select, (((1,), (1,)), ((), ())), preferred_element_type=F32)
    weight_ref[...] = seen[2:3] * ((peers * rows) / count[:, :1])

    def place(stage):
        for d in range(1, peers):
            data_copy(stage, d).wait()
        source = kv_got if stage == 0 else q_got.at[stage - 1]
        width = source.shape[2]
        for p in range(peers):
            padded[p * LANES : p * LANES + room, :width] = source[p]
        return jnp.dot(select[...], padded[:, :width], preferred_element_type=F32).astype(BF16)

    lengths = [jnp.sum(one, axis=1, keepdims=True).astype(jnp.int32) for one in filled]
    kv_slots[...] = place(0)
    for stage in range(q_stages):
        cols = slice(stage * per_stage * DH, (stage + 1) * per_stage * DH)
        q_slots[:, cols] = place(stage + 1)
        heads = range(stage * per_stage, (stage + 1) * per_stage)
        if stage == 0 and wides > 1:
            pass_on(0)
        attend(q_slots, kv_slots, lengths, heads, q_heads // kv_heads, kv_heads, ctx)
        for kind in range(3):
            ctx_copy(stage, kind).start()
        ctx_all[seat, :, cols] = ctx[pl.ds(pl.multiple_of(seat * part, part), part), cols]
    for i in range(1, wides - 1):
        pass_on(i)
    o_load.wait()

    def block(index):
        return ctx[pl.ds(pl.multiple_of(index * part, part), part), :]

    def near_copy(j):
        return pltpu.make_async_remote_copy(
            near_out.at[j], near_in.at[j], near_send.at[j], near_recv.at[j],
            device_id={"seq": partner},
        )

    def mine_copy(j):
        return pltpu.make_async_remote_copy(
            mine_out.at[j], mine_in.at[j], mine_send.at[j], mine_recv.at[j],
            device_id={"seq": partner},
        )

    def far_copy(j):
        return pltpu.make_async_remote_copy(
            far_out.at[j], far_in.at[j], far_send.at[j], far_recv.at[j],
            device_id={"seq": across},
        )

    held = [None] * chunks

    def forward(j):
        near_copy(j).wait()
        far_out[j] = (held[j] + near_in[j].astype(F32)).astype(BF16)
        far_copy(j).start()

    for j in range(chunks):
        w = ow[:, j * chunk : (j + 1) * chunk]
        near_out[j] = jnp.dot(
            block((1 - half) * 2 + (1 - core)), w, preferred_element_type=F32
        ).astype(BF16)
        near_copy(j).start()
        held[j] = jnp.dot(block(across), w, preferred_element_type=F32)
        if j > 0:
            forward(j - 1)
    forward(chunks - 1)
    pass_on(wides - 1)
    for j in range(chunks):
        w = ow[:, j * chunk : (j + 1) * chunk]
        mine_out[j] = jnp.dot(block(partner), w, preferred_element_type=F32).astype(BF16)
        mine_copy(j).start()
        own[:, j * chunk : (j + 1) * chunk] = jnp.dot(
            block(seat), w, preferred_element_type=F32
        )
    for stage in range(q_stages):
        for kind in range(3):
            ctx_copy(stage, kind).wait()
    for i in range(wides):
        wide_copy(0, i).wait()
        wide_copy(2, i).wait()
        total = jnp.zeros((part, chunk), F32)
        for index in range(seq_count):
            total = total + jnp.dot(
                ctx_all[index], wide[index, i], preferred_element_type=F32
            )
        mixed_ref[:, i * chunk : (i + 1) * chunk] = total.astype(BF16)
    for j in range(chunks):
        mine_copy(j).wait()
        cols = slice(j * chunk, (j + 1) * chunk)
        own[:, cols] += mine_in[j].astype(F32)
    for j in range(chunks):
        far_copy(j).wait()
        cols = slice(j * chunk, (j + 1) * chunk)
        mixed_ref[:, (wides + j) * chunk : (wides + j + 1) * chunk] = (
            own[:, cols] + far_in[j].astype(F32)
        ).astype(BF16)


def per_device(
    tokens, positions, loss_mask, sample_tokens, dest_slot, norm_gain,
    q_weight, k_weight, v_weight, q_bias, k_bias, v_bias, o_weight,
):
    peers = lax.axis_size("dp")
    seq_count = lax.axis_size("seq")
    rows, depth = tokens.shape
    slot_count = 2 * BUCKET
    room = -(-(slot_count // peers) // 16) * 16
    group = math.gcd(peers, 8)
    q_heads = q_weight.shape[1] // DH
    kv_heads = k_weight.shape[1] // DH
    per_stage = math.gcd(q_heads, 2)
    stages = q_heads // per_stage
    strips = math.gcd(rows // 16, 4)
    part = slot_count // seq_count
    out_width = o_weight.shape[1]
    chunk = math.gcd(out_width, 512)
    wides = max(1, 3 * (out_width // chunk) // 7)
    chunks = out_width // chunk - wides
    kv_width = 2 * kv_heads * DH
    q_width = per_stage * DH
    vmem = pl.BlockSpec(memory_space=pltpu.VMEM)
    hbm = pl.BlockSpec(memory_space=pl.ANY)
    piece = pltpu.VMEM((chunks, part, chunk), BF16)
    dma = pltpu.SemaphoreType.DMA
    mixed, weight = pl.pallas_call(
        functools.partial(
            layer_kernel, peers, group, seq_count, q_heads, kv_heads, chunk, room, strips
        ),
        in_specs=[
            hbm, vmem, hbm, hbm, hbm, vmem, vmem, vmem, vmem, vmem, vmem, hbm,
        ],
        out_specs=[vmem, vmem],
        out_shape=[
            jax.ShapeDtypeStruct((part, out_width), BF16),
            jax.ShapeDtypeStruct((1, part), F32),
        ],
        scratch_shapes=[
            pltpu.VMEM((rows, depth), BF16),
            pltpu.VMEM((rows, 1), F32),
            pltpu.VMEM(q_weight.shape, BF16),
            pltpu.VMEM((depth, kv_width), BF16),
            pltpu.VMEM((o_weight.shape[0], chunks * chunk), BF16),
            pltpu.VMEM((peers * LANES, rows), BF16),
            pltpu.VMEM((peers, 8, LANES), F32),
            pltpu.VMEM((peers, 8, LANES), F32),
            pltpu.VMEM((stages, peers, room, q_width), BF16),
            pltpu.VMEM((stages, peers, room, q_width), BF16),
            pltpu.VMEM((peers, room, kv_width), BF16),
            pltpu.VMEM((peers, room, kv_width), BF16),
            pltpu.VMEM((slot_count, peers * LANES), BF16),
            pltpu.VMEM((peers * LANES, max(kv_width, q_width)), BF16),
            pltpu.VMEM((slot_count, q_heads * DH), BF16),
            pltpu.VMEM((slot_count, kv_width), BF16),
            pltpu.VMEM((slot_count, q_heads * DH), BF16),
            pltpu.VMEM((part, chunks * chunk), F32),
            piece, piece, piece, piece, piece, piece,
            pltpu.VMEM((rows, DH), F32),
            pltpu.VMEM((rows, DH), F32),
            pltpu.VMEM((seq_count, wides, o_weight.shape[0], chunk), BF16),
            pltpu.VMEM((seq_count, part, q_heads * DH), BF16),
            dma((stages + 1, peers)), dma((stages + 1, peers)), dma((peers,)), dma((peers,)),
            dma((chunks,)), dma((chunks,)), dma((chunks,)),
            dma((chunks,)), dma((chunks,)), dma((chunks,)),
            dma((strips + 4,)), dma((wides,)), dma((3, wides)), dma((3, wides)),
            dma((stages, 3)), dma((stages, 3)),
        ],
        compiler_params=pltpu.CompilerParams(
            collective_id=0, has_side_effects=True, vmem_limit_bytes=67043328
        ),
    )(
        tokens, norm_gain, q_weight, k_weight, v_weight, q_bias, k_bias, v_bias, positions,
        dest_slot, loss_mask, o_weight,
    )
    return (mixed, weight.reshape(part))


def solution(mesh):
    return jax.shard_map(
        per_device,
        mesh=mesh,
        in_specs=(
            P("dp", None),
            P(None, "dp"),
            P("dp"),
            P(),
            P("dp"),
            P(),
            P(None, "seq"),
            P(None, "seq"),
            P(None, "seq"),
            P("seq"),
            P("seq"),
            P("seq"),
            P("seq", None),
        ),
        out_specs=(P(("dp", "seq"), None), P(("dp", "seq"))),
        check_vma=False,
    )
```

profile of v0, /device:TPU:0, one launch (start us, length us, event | category | flops | bytes accessed | tf_op | source)
XLA Modules:
  0.0 74.4 jit_solution(7052332428486847499)
XLA Ops:
  0.6 70.0 %shard_map.131 = (bf16[192,3584]{1,0:T(8,128)(2,1)}, f32[1,192]{1,0:T(1,128)}) custom-call(bf16[576,3584]{1,0:T(8,128)(2,1)} %tok_hbm.1, f32[3584]{0:T(1024)} %gain_ref.1, bf16[3584,512]{1,0:T(8,128)(2,1)} %qw_hbm.1, bf16[3584,128]{1,0:T(8,128)(2,1)} %kw_hbm.1, bf16[3584,128]{1,0:T(8,128)(2,1)} %vw_hbm.1, f32[512]{0:T(512)} %qb_ref.1, f32[128]{0:T(128)} %kb_ref.1, ...), custom_call_target="tpu_custom_call" | custom-call | tf_op jit(solution)/shard_map/pallas_call | solution.py:407
  70.6 2.5 %copy.16 = bf16[192,3584]{1,0:T(8,128)(2,1)} copy(bf16[192,3584]{1,0:T(8,128)(2,1)} %get-tuple-element.8) | data formatting | bytes 2752512
  73.2 1.2 %copy.17 = f32[192]{0:T(256)} copy(f32[192]{0:T(256)} %bitcast.1) | data formatting | bytes 1536
where the time goes:
time: 74.6 us; the launch traced here: 74.4 us
  Pallas kernels  70 us (94%)
  local copies, waits for them, and re-layouts  3.74 us (5%)
    pallas_call x1, Pallas kernels, per_device(): pl.pallas_call(functools.partial(layer_kernel, peers, group, seq_count, q...  70 us
    unnamed x2, local copies, waits for them, and re-layouts  3.74 us

commit v1 on v0

v1 whole, which is shorter than its diff:
```python
import functools
import math

import jax
import jax.numpy as jnp
import numpy as np
from jax import lax
from jax.experimental import pallas as pl
from jax.experimental.pallas import tpu as pltpu
from jax.sharding import PartitionSpec as P

DH = 128
BUCKET = 384
LANES = 128
PIECE = 256
QUADS, X_PAIRS, Z_PAIRS = 1, 2, 1
VMEM_LIMIT = 65000000

NORM_EPSILON = 1e-06
ROPE_BASE = 1000000.0
F32 = jnp.float32
BF16 = jnp.bfloat16


def iota(shape, axis):
    return lax.broadcasted_iota(jnp.int32, shape, axis)


HIGH, LOW = 64, 32
HIGH_ROWS, LOW_ROWS = 256, 128


def turn_tables():
    half_size = DH // 2
    pair = np.arange(half_size, dtype=np.float32)
    freq = np.exp(pair * np.float32(-2.0 * math.log(ROPE_BASE) / DH)).astype(np.float64)
    time_limit = DH // 8
    height_limit = time_limit + 3 * DH // 16
    axis_of = np.where(pair < time_limit, 0, np.where(pair < height_limit, 1, 2))
    sign = np.concatenate([-np.ones(half_size), np.ones(half_size)])
    blocks = []
    for count, step, rows in ((HIGH, LOW, HIGH_ROWS), (LOW, 1, LOW_ROWS)):
        table = np.zeros((rows, 2 * DH))
        for axis in range(3):
            angles = np.arange(count)[:, None] * float(step) * freq[None, :]
            chosen = (axis_of == axis)[None, :]
            cos = np.where(chosen, np.cos(angles), 0.0)
            sin = np.where(chosen, np.sin(angles), 0.0)
            at = slice(axis * count, (axis + 1) * count)
            table[at, :DH] = np.concatenate([cos, cos], axis=1)
            table[at, DH:] = np.concatenate([sin, sin], axis=1) * sign[None, :]
        top = table.astype(jnp.bfloat16)
        rest = (table - top.astype(np.float64)).astype(jnp.bfloat16)
        blocks += [top, rest]
    return np.concatenate(blocks, axis=0)


def rotary_tables(pos_ref, table, cos_out, sin_out):
    ids = pos_ref[...]
    rows = ids.shape[1]
    high = ids // LOW
    low = ids - high * LOW
    kind = iota((8, rows), 0)
    split = jnp.zeros((8, rows), jnp.int32)
    for axis in range(3):
        split = jnp.where(kind == 2 * axis, high[axis : axis + 1], split)
        split = jnp.where(kind == 2 * axis + 1, low[axis : axis + 1], split)
    width = HIGH_ROWS + LOW_ROWS
    column, row = iota((8, width), 1), iota((8, width), 0)
    low_at = column - HIGH_ROWS
    wanted = jnp.where(column < HIGH_ROWS, 2 * (column // HIGH), 2 * (low_at // LOW) + 1)
    spread = jnp.where(row == wanted, 1.0, 0.0).astype(BF16)
    told = lax.dot_general(
        split.astype(F32).astype(BF16), spread, (((0,), (0,)), ((), ())),
        preferred_element_type=F32,
    )
    at = iota((1, width), 1)
    value = jnp.where(
        at < HIGH_ROWS,
        jnp.where(at < 3 * HIGH, at % HIGH, -1),
        jnp.where(at < HIGH_ROWS + 3 * LOW, (at - HIGH_ROWS) % LOW, -1),
    ).astype(F32)
    hot = jnp.where(told == value, 1.0, 0.0).astype(BF16)
    hot_high, hot_low = hot[:, :HIGH_ROWS], hot[:, HIGH_ROWS:]
    low_from = 2 * HIGH_ROWS

    def look(one, first, count):
        return jnp.dot(one, table[first : first + count], preferred_element_type=F32) + jnp.dot(
            one, table[first + count : first + 2 * count], preferred_element_type=F32
        )

    big = look(hot_high, 0, HIGH_ROWS)
    small = look(hot_low, low_from, LOW_ROWS)
    cos_out[...] = big[:, :DH] * small[:, :DH] - big[:, DH:] * small[:, DH:]
    sin_out[...] = big[:, DH:] * small[:, :DH] + big[:, :DH] * small[:, DH:]


def pack_plan(peers, slot_count, group, slot_ref, mask_ref, select_out, info_out):
    rows = slot_ref.shape[0]
    slots = slot_ref[...][None, :]
    peer = slots // slot_count
    local = slots - peer * slot_count + 1
    mask = mask_ref[...][None, :].astype(F32)
    mask_sum = jnp.sum(mask, axis=1, keepdims=True)
    hot = jnp.where(iota((peers, rows), 0) == peer, 1.0, 0.0)
    earlier = jnp.where(iota((rows, rows), 0) < iota((rows, rows), 1), 1.0, 0.0).astype(BF16)
    counts = jnp.dot(hot.astype(BF16), earlier, preferred_element_type=F32)
    rank = jnp.sum(hot * counts, axis=0, keepdims=True).astype(jnp.int32)
    place = peer * LANES + rank
    high = local // 32
    kind = iota((8, rows), 0)
    facts = jnp.where(
        kind == 0,
        high.astype(F32),
        jnp.where(kind == 1, (local - high * 32).astype(F32), jnp.where(kind == 2, mask, 0.0)),
    ).astype(BF16)
    span = group * LANES
    for g in range(peers // group):
        select = jnp.where(iota((span, rows), 0) + g * span == place, 1.0, 0.0).astype(BF16)
        select_out[g * span : (g + 1) * span, :] = select
        told = lax.dot_general(facts, select, (((1,), (1,)), ((), ())), preferred_element_type=F32)
        told = jnp.where(iota(told.shape, 0) == 3, mask_sum, told)
        for p in range(group):
            info_out[g * group + p] = told[:, p * LANES : (p + 1) * LANES]


def attend(q_slots, kv_slots, lengths, heads, per_kv, kv_count, ctx):
    start = 0
    scale = 1.0 / math.sqrt(DH)
    for size, length in zip((BUCKET, BUCKET // 2, BUCKET // 2), lengths):
        rows = slice(start, start + size)
        q_at, k_at = iota((size, size), 0), iota((size, size), 1)
        allowed = (q_at >= k_at) & (k_at < length)
        live = iota((size, DH), 0) < length
        for h in heads:
            pair = h // per_kv
            key = kv_slots[rows, pair * DH : (pair + 1) * DH]
            value = kv_slots[rows, (kv_count + pair) * DH : (kv_count + pair + 1) * DH]
            cols = slice(h * DH, (h + 1) * DH)
            scores = lax.dot_general(
                q_slots[rows, cols], key, (((1,), (1,)), ((), ())), preferred_element_type=F32
            )
            scores = jnp.where(allowed, scores * scale, -1e30)
            top = jnp.max(scores, axis=1, keepdims=True)
            weights = jnp.exp(scores - top)
            total = jnp.sum(weights, axis=1, keepdims=True)
            out = jnp.dot(weights.astype(BF16), value, preferred_element_type=F32) / total
            ctx[rows, cols] = jnp.where(live, out, 0.0).astype(BF16)
        start += size


def layer_kernel(
    peers, group, seq_count, q_heads, kv_heads, chunk, room, strips, pieces,
    tok_hbm, gain_ref, qw_hbm, kw_hbm, vw_hbm, qb_ref, kb_ref, vb_ref, pos_ref,
    slot_ref, mask_ref, ow_hbm, table_hbm,
    mixed_ref, weight_ref,
    x, squares, qw, kvw, ow, table, pick, told_out, got_info, q_out, q_got, kv_out, kv_got,
    select, padded, q_slots, kv_slots, ctx, ctx_far, w_far, held, pair, pair_in,
    far_pair, near_in, far_out, far_in, cos_ref, sin_ref,
    data_send, data_recv, info_send, info_recv, near_send, near_recv,
    pair_send, pair_recv, far_send, far_recv, load_sem,
    y_send, y_recv, x_send, x_recv, z_send, z_recv, ctx_send, ctx_recv,
):
    me = lax.axis_index("dp")
    seat = lax.axis_index("seq")
    half = seat // 2
    core = seat % 2
    partner = half * 2 + (1 - core)
    across = (1 - half) * 2 + core
    a = me % 2
    b = (me // 2) % 2
    x_peer = me + 1 - 2 * a
    z_peer = me + 2 - 4 * b
    q_stages = q_out.shape[0]
    per_stage = q_heads // q_stages
    rows, depth = x.shape
    slot_count = q_slots.shape[0]
    part = slot_count // seq_count
    block_rows = 2 * part
    wide_cols = pieces * PIECE
    out_width = ow.shape[1]
    chunks = (out_width - wide_cols) // chunk
    strip = rows // strips
    kv_cols = kv_heads * DH

    barrier = pltpu.get_barrier_semaphore()
    for d in range(1, peers):
        pl.semaphore_signal(barrier, inc=1, device_id={"dp": (me + d) % peers})
    pl.semaphore_signal(barrier, inc=1, device_id={"seq": partner})
    pl.semaphore_signal(barrier, inc=1, device_id={"seq": across})
    token_loads = [
        pltpu.make_async_copy(
            tok_hbm.at[i * strip : (i + 1) * strip], x.at[i * strip : (i + 1) * strip],
            load_sem.at[i],
        )
        for i in range(strips)
    ]
    k_load = pltpu.make_async_copy(kw_hbm, kvw.at[:, :kv_cols], load_sem.at[strips])
    v_load = pltpu.make_async_copy(vw_hbm, kvw.at[:, kv_cols:], load_sem.at[strips + 1])
    q_load = pltpu.make_async_copy(qw_hbm, qw, load_sem.at[strips + 2])
    o_load = pltpu.make_async_copy(ow_hbm, ow, load_sem.at[strips + 3])
    table_load = pltpu.make_async_copy(table_hbm, table, load_sem.at[strips + 4])
    for copy in [table_load] + token_loads + [k_load, v_load, q_load, o_load]:
        copy.start()

    y_own, x_jobs, z_jobs = [], [], []
    for k in range(QUADS):
        own = 4 * k + 2 * b + a
        y_at = len(y_own)
        y_own.append(own)
        z_at = len(z_jobs)
        z_jobs.append((own, y_at))
        x_jobs.append((own, "y", y_at))
        x_jobs.append((4 * k + 2 * (1 - b) + a, "z", z_at))
    for k in range(X_PAIRS):
        own = 4 * QUADS + 2 * k + a
        x_jobs.append((own, "y", len(y_own)))
        y_own.append(own)
    for k in range(Z_PAIRS):
        own = 4 * QUADS + 2 * X_PAIRS + 2 * k + b
        z_jobs.append((own, len(y_own)))
        y_own.append(own)

    def y_copy(i):
        at = pl.multiple_of(y_own[i] * PIECE, PIECE)
        return pltpu.make_async_remote_copy(
            ow_hbm.at[:, pl.ds(at, PIECE)], w_far.at[y_own[i]], y_send.at[i], y_recv.at[i],
            device_id={"seq": across},
        )

    def x_copy(i):
        own = x_jobs[i][0]
        return pltpu.make_async_remote_copy(
            w_far.at[own], w_far.at[own], x_send.at[i], x_recv.at[i], device_id={"dp": x_peer}
        )

    def z_copy(i):
        own = z_jobs[i][0]
        return pltpu.make_async_remote_copy(
            w_far.at[own], w_far.at[own], z_send.at[i], z_recv.at[i], device_id={"dp": z_peer}
        )

    def from_y(i):
        y_copy(i).wait_recv()
        for n, (_, source, at) in enumerate(x_jobs):
            if source == "y" and at == i:
                x_copy(n).start()
        for n, (_, at) in enumerate(z_jobs):
            if at == i:
                z_copy(n).start()

    def from_z(i):
        z_copy(i).wait_recv()
        for n, (_, source, at) in enumerate(x_jobs):
            if source == "z" and at == i:
                x_copy(n).start()

    pack_plan(peers, slot_count, group, slot_ref, mask_ref, pick, told_out)
    gain = gain_ref[...][None, :]
    for i in range(strips):
        token_loads[i].wait()
        at = slice(i * strip, (i + 1) * strip)
        total = jnp.zeros((strip, LANES), F32)
        for c in range(depth // LANES):
            cols = slice(c * LANES, (c + 1) * LANES)
            entry = x[at, cols].astype(F32)
            total = total + entry * entry
            x[at, cols] = (entry * gain[:, cols]).astype(BF16)
        squares[at, :] = jnp.sum(total, axis=1, keepdims=True)
    inverse = lax.rsqrt(squares[...] * (1.0 / depth) + NORM_EPSILON)

    def info_copy(d):
        to = (me + d) % peers
        return pltpu.make_async_remote_copy(
            told_out.at[to], got_info.at[me], info_send.at[d], info_recv.at[d],
            device_id={"dp": to},
        )

    def ctx_copy(stage):
        cols = slice(stage * per_stage * DH, (stage + 1) * per_stage * DH)
        return pltpu.make_async_remote_copy(
            ctx.at[pl.ds(pl.multiple_of((1 - half) * block_rows, block_rows), block_rows), cols],
            ctx_far.at[:, cols], ctx_send.at[stage], ctx_recv.at[stage],
            device_id={"seq": across},
        )

    def data_copy(stage, d):
        to = (me + d) % peers
        source, target = (kv_out, kv_got) if stage == 0 else (q_out, q_got)
        if stage > 0:
            source, target = source.at[stage - 1], target.at[stage - 1]
        return pltpu.make_async_remote_copy(
            source.at[to], target.at[me], data_send.at[stage, d], data_recv.at[stage, d],
            device_id={"dp": to},
        )

    def turn(wide):
        return wide * cos_ref[...] + pltpu.roll(wide, DH // 2, 1) * sin_ref[...]

    def pack(stage, values):
        span = group * LANES
        target, kept = (kv_out, kv_got) if stage == 0 else (q_out, q_got)
        if stage > 0:
            target, kept = target.at[stage - 1], kept.at[stage - 1]
        for g in range(peers // group):
            moved = jnp.dot(
                pick[g * span : (g + 1) * span, :], values, preferred_element_type=F32
            ).astype(BF16)
            for p in range(group):
                target[g * group + p] = moved[p * LANES : p * LANES + room]
        for d in range(1, peers):
            data_copy(stage, d).start()
        kept[me] = target[me]

    pl.semaphore_wait(barrier, peers + 1)
    for i in range(len(y_own)):
        y_copy(i).start()
    for d in range(1, peers):
        info_copy(d).start()
    got_info[me] = told_out[me]
    table_load.wait()
    rotary_tables(pos_ref, table, cos_ref, sin_ref)
    k_load.wait()
    v_load.wait()
    product = jnp.dot(x[...], kvw[...], preferred_element_type=F32)
    heads_out = []
    for h in range(2 * kv_heads):
        bias_ref, at = (kb_ref, h) if h < kv_heads else (vb_ref, h - kv_heads)
        bias = bias_ref[at * DH : (at + 1) * DH][None, :]
        head = (product[:, h * DH : (h + 1) * DH] * inverse + bias).astype(BF16)
        if h < kv_heads:
            head = turn(head.astype(F32)).astype(BF16)
        heads_out.append(head)
    pack(0, jnp.concatenate(heads_out, axis=1))
    q_load.wait()
    for stage in range(q_stages):
        cols = slice(stage * per_stage * DH, (stage + 1) * per_stage * DH)
        product = jnp.dot(x[...], qw[:, cols], preferred_element_type=F32)
        heads_out = []
        for i in range(per_stage):
            h = stage * per_stage + i
            bias = qb_ref[h * DH : (h + 1) * DH][None, :]
            head = (product[:, i * DH : (i + 1) * DH] * inverse + bias).astype(BF16)
            heads_out.append(turn(head.astype(F32)).astype(BF16))
        pack(stage + 1, jnp.concatenate(heads_out, axis=1))

    padded[...] = jnp.zeros_like(padded)
    for d in range(1, peers):
        info_copy(d).wait()
    count = jnp.zeros((1, LANES), F32)
    slot_at = iota((slot_count, LANES), 0).astype(F32)
    facts = []
    filled = [jnp.zeros((1, LANES), F32) for _ in range(3)]
    starts = (0, BUCKET, BUCKET + BUCKET // 2, 2 * BUCKET)
    for p in range(peers):
        told = got_info[p]
        facts.append(told)
        count = count + told[3:4]
        local = told[0:1] * 32.0 + told[1:2] - 1.0
        for bucket in range(3):
            inside = (local >= float(starts[bucket])) & (local < float(starts[bucket + 1]))
            filled[bucket] = filled[bucket] + jnp.where(inside, 1.0, 0.0)
        select[:, p * LANES : (p + 1) * LANES] = jnp.where(slot_at == local, 1.0, 0.0).astype(BF16)
    flags = jnp.concatenate(facts, axis=1).astype(BF16)
    own_select = select[pl.ds(pl.multiple_of(seat * part, part), part), :]
    seen = lax.dot_general(flags, own_select, (((1,), (1,)), ((), ())), preferred_element_type=F32)
    weight_ref[...] = seen[2:3] * ((peers * rows) / count[:, :1])

    def place(stage):
        for d in range(1, peers):
            data_copy(stage, d).wait()
        source = kv_got if stage == 0 else q_got.at[stage - 1]
        width = source.shape[2]
        for p in range(peers):
            padded[p * LANES : p * LANES + room, :width] = source[p]
        return jnp.dot(select[...], padded[:, :width], preferred_element_type=F32).astype(BF16)

    lengths = [jnp.sum(one, axis=1, keepdims=True).astype(jnp.int32) for one in filled]
    y_next = 0
    z_next = 0
    y_count, z_count = len(y_own), len(z_jobs)
    steps = q_stages + 1
    for stage in range(steps):
        while y_next < (stage + 1) * y_count // steps:
            from_y(y_next)
            y_next += 1
        if stage == 0:
            kv_slots[...] = place(0)
            continue
        while z_next < (stage * QUADS) // q_stages:
            from_z(z_next)
            z_next += 1
        q_at = stage - 1
        cols = slice(q_at * per_stage * DH, (q_at + 1) * per_stage * DH)
        q_slots[:, cols] = place(stage)
        heads = range(q_at * per_stage, (q_at + 1) * per_stage)
        attend(q_slots, kv_slots, lengths, heads, q_heads // kv_heads, kv_heads, ctx)
        ctx_copy(q_at).start()
    o_load.wait()

    def near_copy(j):
        to_row = pl.multiple_of((1 - core) * part, part)
        cols = slice(j * chunk, (j + 1) * chunk)
        return pltpu.make_async_remote_copy(
            far_pair.at[pl.ds(to_row, part), cols], near_in.at[:, cols],
            near_send.at[j], near_recv.at[j], device_id={"seq": partner},
        )

    def far_copy(j):
        cols = slice(j * chunk, (j + 1) * chunk)
        return pltpu.make_async_remote_copy(
            far_out.at[:, cols], far_in.at[:, cols], far_send.at[j], far_recv.at[j],
            device_id={"seq": across},
        )

    groups = [(i * PIECE, PIECE) for i in range(pieces)]
    groups += [(wide_cols + j * chunk, chunk) for j in range(chunks)]

    def pair_copy(n):
        first, width = groups[n]
        to_row = pl.multiple_of((1 - core) * part, part)
        return pltpu.make_async_remote_copy(
            pair.at[pl.ds(to_row, part), first : first + width],
            pair_in.at[:, first : first + width],
            pair_send.at[n], pair_recv.at[n], device_id={"seq": partner},
        )

    mine_at = pl.multiple_of(half * block_rows, block_rows)
    far_at = pl.multiple_of((1 - half) * block_rows, block_rows)
    own_at = pl.multiple_of(core * part, part)

    def forward(j):
        near_copy(j).wait_recv()
        cols = slice(j * chunk, (j + 1) * chunk)
        kept = far_pair[pl.ds(own_at, part), cols].astype(F32)
        far_out[:, cols] = (kept + near_in[:, cols].astype(F32)).astype(BF16)
        far_copy(j).start()

    for j in range(chunks):
        cols = slice(j * chunk, (j + 1) * chunk)
        w = ow[:, wide_cols + j * chunk : wide_cols + (j + 1) * chunk]
        far_pair[:, cols] = jnp.dot(
            ctx[pl.ds(far_at, block_rows), :], w, preferred_element_type=F32
        ).astype(BF16)
        near_copy(j).start()
        if j > 0:
            forward(j - 1)
    if chunks:
        forward(chunks - 1)
    for j in range(chunks):
        first, width = groups[pieces + j]
        pair[:, first : first + width] = jnp.dot(
            ctx[pl.ds(mine_at, block_rows), :], ow[:, first : first + width],
            preferred_element_type=F32,
        ).astype(BF16)
        pair_copy(pieces + j).start()
    for i in range(pieces):
        held[:, i * PIECE : (i + 1) * PIECE] = jnp.dot(
            ctx[pl.ds(mine_at, block_rows), :], ow[:, i * PIECE : (i + 1) * PIECE],
            preferred_element_type=F32,
        )
    for stage in range(q_stages):
        ctx_copy(stage).wait()
    for i in range(y_count):
        y_copy(i).wait_send()

    def finish(i):
        cols = slice(i * PIECE, (i + 1) * PIECE)
        pair[:, cols] = (
            held[:, cols] + jnp.dot(ctx_far[...], w_far[i], preferred_element_type=F32)
        ).astype(BF16)
        pair_copy(i).start()

    for k in range(X_PAIRS):
        x_copy(2 * QUADS + k).wait()
        finish(4 * QUADS + 2 * k)
        finish(4 * QUADS + 2 * k + 1)
    for k in range(Z_PAIRS):
        z_copy(QUADS + k).wait()
        finish(4 * QUADS + 2 * X_PAIRS + 2 * k)
        finish(4 * QUADS + 2 * X_PAIRS + 2 * k + 1)
    for k in range(QUADS):
        z_copy(k).wait_send()
        x_copy(2 * k).wait()
        x_copy(2 * k + 1).wait()
        for i in range(4 * k, 4 * k + 4):
            finish(i)
    for n in list(range(pieces, pieces + chunks)) + list(range(pieces)):
        first, width = groups[n]
        cols = slice(first, first + width)
        pair_copy(n).wait()
        total = pair[pl.ds(own_at, part), cols].astype(F32) + pair_in[:, cols].astype(F32)
        if n >= pieces:
            j = n - pieces
            near_copy(j).wait_send()
            far_copy(j).wait()
            total = total + far_in[:, j * chunk : (j + 1) * chunk].astype(F32)
        mixed_ref[:, cols] = total.astype(BF16)


def deliver(mixed_in, weight_in, mixed_hbm, weight_hbm, flat, sems):
    big = pltpu.make_async_copy(mixed_in, mixed_hbm, sems.at[0])
    big.start()
    flat[...] = weight_in[0, :]
    small = pltpu.make_async_copy(flat, weight_hbm, sems.at[1])
    small.start()
    big.wait()
    small.wait()


def per_device(
    tokens, positions, loss_mask, sample_tokens, dest_slot, norm_gain,
    q_weight, k_weight, v_weight, q_bias, k_bias, v_bias, o_weight,
):
    peers = lax.axis_size("dp")
    seq_count = lax.axis_size("seq")
    rows, depth = tokens.shape
    slot_count = 2 * BUCKET
    room = -(-(slot_count // peers) // 16) * 16
    group = math.gcd(peers, 8)
    q_heads = q_weight.shape[1] // DH
    kv_heads = k_weight.shape[1] // DH
    per_stage = math.gcd(q_heads, 2)
    stages = q_heads // per_stage
    strips = math.gcd(rows // 16, 4)
    part = slot_count // seq_count
    out_width = o_weight.shape[1]
    pieces = 4 * QUADS + 2 * X_PAIRS + 2 * Z_PAIRS
    wide_cols = pieces * PIECE
    narrow = out_width - wide_cols
    chunk = math.gcd(narrow, 512)
    chunks = narrow // chunk
    kv_width = 2 * kv_heads * DH
    q_width = per_stage * DH
    y_count = QUADS + X_PAIRS + Z_PAIRS
    x_count = 2 * QUADS + X_PAIRS
    z_count = QUADS + Z_PAIRS
    vmem = pl.BlockSpec(memory_space=pltpu.VMEM)
    hbm = pl.BlockSpec(memory_space=pl.ANY)
    dma = pltpu.SemaphoreType.DMA
    table = turn_tables()
    mixed, weight = pl.pallas_call(
        functools.partial(
            layer_kernel, peers, group, seq_count, q_heads, kv_heads, chunk, room, strips, pieces
        ),
        in_specs=[
            hbm, vmem, hbm, hbm, hbm, vmem, vmem, vmem, vmem, vmem, vmem, hbm, hbm,
        ],
        out_specs=[vmem, vmem],
        out_shape=[
            jax.ShapeDtypeStruct((part, out_width), BF16),
            jax.ShapeDtypeStruct((1, part), F32),
        ],
        scratch_shapes=[
            pltpu.VMEM((rows, depth), BF16),
            pltpu.VMEM((rows, 1), F32),
            pltpu.VMEM(q_weight.shape, BF16),
            pltpu.VMEM((depth, kv_width), BF16),
            pltpu.VMEM(o_weight.shape, BF16),
            pltpu.VMEM(table.shape, BF16),
            pltpu.VMEM((peers * LANES, rows), BF16),
            pltpu.VMEM((peers, 8, LANES), F32),
            pltpu.VMEM((peers, 8, LANES), F32),
            pltpu.VMEM((stages, peers, room, q_width), BF16),
            pltpu.VMEM((stages, peers, room, q_width), BF16),
            pltpu.VMEM((peers, room, kv_width), BF16),
            pltpu.VMEM((peers, room, kv_width), BF16),
            pltpu.VMEM((slot_count, peers * LANES), BF16),
            pltpu.VMEM((peers * LANES, max(kv_width, q_width)), BF16),
            pltpu.VMEM((slot_count, q_heads * DH), BF16),
            pltpu.VMEM((slot_count, kv_width), BF16),
            pltpu.VMEM((slot_count, q_heads * DH), BF16),
            pltpu.VMEM((2 * part, q_heads * DH), BF16),
            pltpu.VMEM((pieces, o_weight.shape[0], PIECE), BF16),
            pltpu.VMEM((2 * part, wide_cols), F32),
            pltpu.VMEM((2 * part, out_width), BF16),
            pltpu.VMEM((part, out_width), BF16),
            pltpu.VMEM((2 * part, narrow), BF16),
            pltpu.VMEM((part, narrow), BF16),
            pltpu.VMEM((part, narrow), BF16),
            pltpu.VMEM((part, narrow), BF16),
            pltpu.VMEM((rows, DH), F32),
            pltpu.VMEM((rows, DH), F32),
            dma((stages + 1, peers)), dma((stages + 1, peers)), dma((peers,)), dma((peers,)),
            dma((chunks,)), dma((chunks,)), dma((pieces + chunks,)), dma((pieces + chunks,)),
            dma((chunks,)), dma((chunks,)), dma((strips + 5,)),
            dma((y_count,)), dma((y_count,)), dma((x_count,)), dma((x_count,)),
            dma((z_count,)), dma((z_count,)), dma((stages,)), dma((stages,)),
        ],
        compiler_params=pltpu.CompilerParams(
            collective_id=0, has_side_effects=True, vmem_limit_bytes=VMEM_LIMIT
        ),
    )(
        tokens, norm_gain, q_weight, k_weight, v_weight, q_bias, k_bias, v_bias, positions,
        dest_slot, loss_mask, o_weight, jnp.asarray(table),
    )
    return pl.pallas_call(
        deliver,
        in_specs=[vmem, vmem],
        out_specs=[hbm, hbm],
        out_shape=[
            jax.ShapeDtypeStruct((part, out_width), BF16),
            jax.ShapeDtypeStruct((part,), F32),
        ],
        scratch_shapes=[pltpu.VMEM((part,), F32), dma((2,))],
    )(mixed, weight)


def solution(mesh):
    return jax.shard_map(
        per_device,
        mesh=mesh,
        in_specs=(
            P("dp", None),
            P(None, "dp"),
            P("dp"),
            P(),
            P("dp"),
            P(),
            P(None, "seq"),
            P(None, "seq"),
            P(None, "seq"),
            P("seq"),
            P("seq"),
            P("seq"),
            P("seq", None),
        ),
        out_specs=(P(("dp", "seq"), None), P(("dp", "seq"))),
        check_vma=False,
    )
```

time: 74.6 us -> 58.5 us (0.78)
  Pallas kernels: 70 us -> 57.5 us
  local copies, waits for them, and re-layouts: 3.74 us -> 0 us
    pallas_call x1, Pallas kernels: 70 us -> 55.1 us  [per_device(): pl.pallas_call(functools.partial(layer_kernel, peers, group, seq_count, q...]
    unnamed x2 -> x0, local copies, waits for them, and re-layouts: 3.74 us -> none
    pallas_call x0 -> x1, Pallas kernels: none -> 2.44 us  [per_device(): pl.pallas_call(deliver, in_specs=[vmem, vmem], out_specs=[hbm, hbm], out_...]
where the time goes in v1:
time: 58.5 us; the launch traced here: 58.3 us
  Pallas kernels  57.5 us (98%)
  between operations  0.8 us (1%)
    pallas_call x1, Pallas kernels, per_device(): pl.pallas_call(functools.partial(layer_kernel, peers, group, seq_count, q...  55.1 us
    pallas_call x1, Pallas kernels, per_device(): pl.pallas_call(deliver, in_specs=[vmem, vmem], out_specs=[hbm, hbm], out_...  2.44 us

profile of v1, /device:TPU:0, one launch (start us, length us, event | category | flops | bytes accessed | tf_op | source)
XLA Modules:
  0.0 58.3 jit_solution(18092805672065868809)
XLA Ops:
  0.6 55.1 %shard_map.140 = (bf16[192,3584]{1,0:T(8,128)(2,1)}, f32[1,192]{1,0:T(1,128)}) custom-call(bf16[576,3584]{1,0:T(8,128)(2,1)} %tok_hbm.1, f32[3584]{0:T(1024)} %gain_ref.1, bf16[3584,512]{1,0:T(8,128)(2,1)} %qw_hbm.1, bf16[3584,128]{1,0:T(8,128)(2,1)} %kw_hbm.1, bf16[3584,128]{1,0:T(8,128)(2,1)} %vw_hbm.1, f32[512]{0:T(512)} %qb_ref.1, f32[128]{0:T(128)} %kb_ref.1, ...), custom_call_target="tpu_custom_call" | custom-call | tf_op jit(solution)/shard_map/pallas_call | solution.py:542
  55.7 2.4 %shard_map.141 = (bf16[192,3584]{1,0:T(8,128)(2,1)}, f32[192]{0:T(256)}) custom-call(bf16[192,3584]{1,0:T(8,128)(2,1)} %get-tuple-element.4.mixed_in, f32[1,192]{1,0:T(1,128)} %get-tuple-element.5.weight_in), custom_call_target="tpu_custom_call" | custom-call | tf_op jit(solution)/shard_map/pallas_call | solution.py:597

commit v2 on v1

--- a/solution.py
+++ b/solution.py
@@ -14,7 +14,8 @@
 LANES = 128
 PIECE = 256
 QUADS, X_PAIRS, Z_PAIRS = 1, 2, 1
-VMEM_LIMIT = 65000000
+Y_AT, Z_AT = 0, 3
+VMEM_LIMIT = 52000000
 
 NORM_EPSILON = 1e-06
 ROPE_BASE = 1000000.0
@@ -95,7 +96,7 @@
     sin_out[...] = big[:, DH:] * small[:, :DH] + big[:, :DH] * small[:, DH:]
 
 
-def pack_plan(peers, slot_count, group, slot_ref, mask_ref, select_out, info_out):
+def pack_plan(peers, slot_count, group, room, slot_ref, mask_ref, select_out, info_out):
     rows = slot_ref.shape[0]
     slots = slot_ref[...][None, :]
     peer = slots // slot_count
@@ -106,7 +107,7 @@
     earlier = jnp.where(iota((rows, rows), 0) < iota((rows, rows), 1), 1.0, 0.0).astype(BF16)
     counts = jnp.dot(hot.astype(BF16), earlier, preferred_element_type=F32)
     rank = jnp.sum(hot * counts, axis=0, keepdims=True).astype(jnp.int32)
-    place = peer * LANES + rank
+    place = peer * room + rank
     high = local // 32
     kind = iota((8, rows), 0)
     facts = jnp.where(
@@ -114,14 +115,16 @@
         high.astype(F32),
         jnp.where(kind == 1, (local - high * 32).astype(F32), jnp.where(kind == 2, mask, 0.0)),
     ).astype(BF16)
-    span = group * LANES
+    span = group * room
+    spare = jnp.zeros((8, LANES - room), F32)
     for g in range(peers // group):
         select = jnp.where(iota((span, rows), 0) + g * span == place, 1.0, 0.0).astype(BF16)
         select_out[g * span : (g + 1) * span, :] = select
         told = lax.dot_general(facts, select, (((1,), (1,)), ((), ())), preferred_element_type=F32)
         told = jnp.where(iota(told.shape, 0) == 3, mask_sum, told)
         for p in range(group):
-            info_out[g * group + p] = told[:, p * LANES : (p + 1) * LANES]
+            one = told[:, p * room : (p + 1) * room]
+            info_out[g * group + p] = jnp.concatenate([one, spare], axis=1)
 
 
 def attend(q_slots, kv_slots, lengths, heads, per_kv, kv_count, ctx):
@@ -151,15 +154,16 @@
 
 def layer_kernel(
     peers, group, seq_count, q_heads, kv_heads, chunk, room, strips, pieces,
-    tok_hbm, gain_ref, qw_hbm, kw_hbm, vw_hbm, qb_ref, kb_ref, vb_ref, pos_ref,
-    slot_ref, mask_ref, ow_hbm, table_hbm,
+    tok_hbm, gain_hbm, qw_hbm, kw_hbm, vw_hbm, qb_hbm, kb_hbm, vb_hbm, pos_hbm,
+    slot_hbm, mask_hbm, ow_hbm, table_hbm,
     mixed_ref, weight_ref,
     x, squares, qw, kvw, ow, table, pick, told_out, got_info, q_out, q_got, kv_out, kv_got,
-    select, padded, q_slots, kv_slots, ctx, ctx_far, w_far, held, pair, pair_in,
-    far_pair, near_in, far_out, far_in, cos_ref, sin_ref,
+    gain_ref, qb_ref, kb_ref, vb_ref, pos_ref, slot_ref, mask_ref,
+    select, q_slots, kv_slots, ctx, ctx_far, w_far, held, pair, pair_in,
+    far_pair, near_in, far_out, far_in, cos_ref, sin_ref, product,
     data_send, data_recv, info_send, info_recv, near_send, near_recv,
     pair_send, pair_recv, far_send, far_recv, load_sem,
-    y_send, y_recv, x_send, x_recv, z_send, z_recv, ctx_send, ctx_recv,
+    y_send, y_recv, x_send, x_recv, z_send, z_recv, ctx_send, ctx_recv, small_sem,
 ):
     me = lax.axis_index("dp")
     seat = lax.axis_index("seq")
@@ -171,8 +175,7 @@
     b = (me // 2) % 2
     x_peer = me + 1 - 2 * a
     z_peer = me + 2 - 4 * b
-    q_stages = q_out.shape[0]
-    per_stage = q_heads // q_stages
+    together = math.gcd(q_heads, 2)
     rows, depth = x.shape
     slot_count = q_slots.shape[0]
     part = slot_count // seq_count
@@ -200,7 +203,16 @@
     q_load = pltpu.make_async_copy(qw_hbm, qw, load_sem.at[strips + 2])
     o_load = pltpu.make_async_copy(ow_hbm, ow, load_sem.at[strips + 3])
     table_load = pltpu.make_async_copy(table_hbm, table, load_sem.at[strips + 4])
-    for copy in [table_load] + token_loads + [k_load, v_load, q_load, o_load]:
+    small_loads = [
+        pltpu.make_async_copy(source, target, small_sem.at[i])
+        for i, (source, target) in enumerate(
+            (
+                (slot_hbm, slot_ref), (mask_hbm, mask_ref), (pos_hbm, pos_ref),
+                (gain_hbm, gain_ref), (kb_hbm, kb_ref), (vb_hbm, vb_ref), (qb_hbm, qb_ref),
+            )
+        )
+    ]
+    for copy in small_loads + [table_load] + token_loads + [k_load, v_load]:
         copy.start()
 
     y_own, x_jobs, z_jobs = [], [], []
@@ -255,10 +267,67 @@
             if source == "z" and at == i:
                 x_copy(n).start()
 
-    pack_plan(peers, slot_count, group, slot_ref, mask_ref, pick, told_out)
+    small_loads[0].wait()
+    small_loads[1].wait()
+    pack_plan(peers, slot_count, group, room, slot_ref, mask_ref, pick, told_out)
+    for copy in small_loads[2:]:
+        copy.wait()
+    table_load.wait()
+    rotary_tables(pos_ref, table, cos_ref, sin_ref)
     gain = gain_ref[...][None, :]
-    for i in range(strips):
-        token_loads[i].wait()
+
+    def info_copy(d):
+        to = (me + d) % peers
+        return pltpu.make_async_remote_copy(
+            told_out.at[to], got_info.at[me], info_send.at[d], info_recv.at[d],
+            device_id={"dp": to},
+        )
+
+    def ctx_copy(h):
+        cols = slice(h * DH, (h + 1) * DH)
+        return pltpu.make_async_remote_copy(
+            ctx.at[pl.ds(pl.multiple_of((1 - half) * block_rows, block_rows), block_rows), cols],
+            ctx_far.at[:, cols], ctx_send.at[h], ctx_recv.at[h],
+            device_id={"seq": across},
+        )
+
+    def data_copy(stage, d):
+        to = (me + d) % peers
+        source, target = (kv_out, kv_got) if stage == 0 else (q_out, q_got)
+        if stage > 0:
+            source, target = source.at[stage - 1], target.at[stage - 1]
+        return pltpu.make_async_remote_copy(
+            source.at[to], target.at[me], data_send.at[stage, d], data_recv.at[stage, d],
+            device_id={"dp": to},
+        )
+
+    def turn(wide):
+        return wide * cos_ref[...] + pltpu.roll(wide, DH // 2, 1) * sin_ref[...]
+
+    def pack(values, targets):
+        span = group * room
+        for g in range(peers // group):
+            moved = jnp.dot(
+                pick[g * span : (g + 1) * span, :], values, preferred_element_type=F32
+            ).astype(BF16)
+            first = 0
+            for target in targets:
+                width = target.shape[2]
+                for p in range(group):
+                    target[g * group + p] = moved[
+                        p * room : (p + 1) * room, first : first + width
+                    ]
+                first += width
+
+    def send(stage):
+        for d in range(1, peers):
+            data_copy(stage, d).start()
+        source, kept = (kv_out, kv_got) if stage == 0 else (q_out, q_got)
+        if stage > 0:
+            source, kept = source.at[stage - 1], kept.at[stage - 1]
+        kept[me] = source[me]
+
+    def norm(i):
         at = slice(i * strip, (i + 1) * strip)
         total = jnp.zeros((strip, LANES), F32)
         for c in range(depth // LANES):
@@ -267,62 +336,21 @@
             total = total + entry * entry
             x[at, cols] = (entry * gain[:, cols]).astype(BF16)
         squares[at, :] = jnp.sum(total, axis=1, keepdims=True)
-    inverse = lax.rsqrt(squares[...] * (1.0 / depth) + NORM_EPSILON)
-
-    def info_copy(d):
-        to = (me + d) % peers
-        return pltpu.make_async_remote_copy(
-            told_out.at[to], got_info.at[me], info_send.at[d], info_recv.at[d],
-            device_id={"dp": to},
-        )
-
-    def ctx_copy(stage):
-        cols = slice(stage * per_stage * DH, (stage + 1) * per_stage * DH)
-        return pltpu.make_async_remote_copy(
-            ctx.at[pl.ds(pl.multiple_of((1 - half) * block_rows, block_rows), block_rows), cols],
-            ctx_far.at[:, cols], ctx_send.at[stage], ctx_recv.at[stage],
-            device_id={"seq": across},
-        )
-
-    def data_copy(stage, d):
-        to = (me + d) % peers
-        source, target = (kv_out, kv_got) if stage == 0 else (q_out, q_got)
-        if stage > 0:
-            source, target = source.at[stage - 1], target.at[stage - 1]
-        return pltpu.make_async_remote_copy(
-            source.at[to], target.at[me], data_send.at[stage, d], data_recv.at[stage, d],
-            device_id={"dp": to},
-        )
-
-    def turn(wide):
-        return wide * cos_ref[...] + pltpu.roll(wide, DH // 2, 1) * sin_ref[...]
-
-    def pack(stage, values):
-        span = group * LANES
-        target, kept = (kv_out, kv_got) if stage == 0 else (q_out, q_got)
-        if stage > 0:
-            target, kept = target.at[stage - 1], kept.at[stage - 1]
-        for g in range(peers // group):
-            moved = jnp.dot(
-                pick[g * span : (g + 1) * span, :], values, preferred_element_type=F32
-            ).astype(BF16)
-            for p in range(group):
-                target[g * group + p] = moved[p * LANES : p * LANES + room]
-        for d in range(1, peers):
-            data_copy(stage, d).start()
-        kept[me] = target[me]
-
-    pl.semaphore_wait(barrier, peers + 1)
-    for i in range(len(y_own)):
-        y_copy(i).start()
-    for d in range(1, peers):
-        info_copy(d).start()
-    got_info[me] = told_out[me]
-    table_load.wait()
-    rotary_tables(pos_ref, table, cos_ref, sin_ref)
+
+    for i in range(strips // 2):
+        token_loads[i].wait()
+        norm(i)
+    for i in range(strips // 2, strips):
+        token_loads[i].wait()
     k_load.wait()
     v_load.wait()
-    product = jnp.dot(x[...], kvw[...], preferred_element_type=F32)
+    q_load.start()
+    top = strips // 2 * strip
+    for i in range(strips // 2, strips):
+        norm(i)
+    product[:top] = jnp.dot(x[:top], kvw[...], preferred_element_type=F32)
+    product[top:] = jnp.dot(x[top:], kvw[...], preferred_element_type=F32)
+    inverse = lax.rsqrt(squares[...] * (1.0 / depth) + NORM_EPSILON)
     heads_out = []
     for h in range(2 * kv_heads):
         bias_ref, at = (kb_ref, h) if h < kv_heads else (vb_ref, h - kv_heads)
@@ -331,71 +359,75 @@
         if h < kv_heads:
             head = turn(head.astype(F32)).astype(BF16)
         heads_out.append(head)
-    pack(0, jnp.concatenate(heads_out, axis=1))
+    pack(jnp.concatenate(heads_out, axis=1), [kv_out])
+    pl.semaphore_wait(barrier, peers + 1)
+    send(0)
+    for i in range(len(y_own)):
+        y_copy(i).start()
+    for d in range(1, peers):
+        info_copy(d).start()
+    got_info[me] = told_out[me]
     q_load.wait()
-    for stage in range(q_stages):
-        cols = slice(stage * per_stage * DH, (stage + 1) * per_stage * DH)
-        product = jnp.dot(x[...], qw[:, cols], preferred_element_type=F32)
+    o_load.start()
+    for first in range(0, q_heads, together):
+        cols = slice(first * DH, (first + together) * DH)
+        made = jnp.dot(x[...], qw[:, cols], preferred_element_type=F32)
         heads_out = []
-        for i in range(per_stage):
-            h = stage * per_stage + i
+        for i in range(together):
+            h = first + i
             bias = qb_ref[h * DH : (h + 1) * DH][None, :]
-            head = (product[:, i * DH : (i + 1) * DH] * inverse + bias).astype(BF16)
+            head = (made[:, i * DH : (i + 1) * DH] * inverse + bias).astype(BF16)
             heads_out.append(turn(head.astype(F32)).astype(BF16))
-        pack(stage + 1, jnp.concatenate(heads_out, axis=1))
-
-    padded[...] = jnp.zeros_like(padded)
+        pack(
+            jnp.concatenate(heads_out, axis=1), [q_out.at[first + i] for i in range(together)]
+        )
+        for i in range(together):
+            send(first + i + 1)
+
     for d in range(1, peers):
         info_copy(d).wait()
-    count = jnp.zeros((1, LANES), F32)
-    slot_at = iota((slot_count, LANES), 0).astype(F32)
-    facts = []
-    filled = [jnp.zeros((1, LANES), F32) for _ in range(3)]
+    facts = jnp.concatenate([got_info[p][:, :room] for p in range(peers)], axis=1)
+    count = jnp.zeros((1, 1), F32)
+    for p in range(peers):
+        count = count + got_info[p][3:4, :1]
+    local = facts[0:1] * 32.0 + facts[1:2] - 1.0
     starts = (0, BUCKET, BUCKET + BUCKET // 2, 2 * BUCKET)
-    for p in range(peers):
-        told = got_info[p]
-        facts.append(told)
-        count = count + told[3:4]
-        local = told[0:1] * 32.0 + told[1:2] - 1.0
-        for bucket in range(3):
-            inside = (local >= float(starts[bucket])) & (local < float(starts[bucket + 1]))
-            filled[bucket] = filled[bucket] + jnp.where(inside, 1.0, 0.0)
-        select[:, p * LANES : (p + 1) * LANES] = jnp.where(slot_at == local, 1.0, 0.0).astype(BF16)
-    flags = jnp.concatenate(facts, axis=1).astype(BF16)
+    lengths = []
+    for bucket in range(3):
+        inside = (local >= float(starts[bucket])) & (local < float(starts[bucket + 1]))
+        filled = jnp.sum(jnp.where(inside, 1.0, 0.0), axis=1, keepdims=True)
+        lengths.append(filled.astype(jnp.int32))
+    slot_at = iota((slot_count, peers * room), 0).astype(F32)
+    select[...] = jnp.where(slot_at == local, 1.0, 0.0).astype(BF16)
     own_select = select[pl.ds(pl.multiple_of(seat * part, part), part), :]
-    seen = lax.dot_general(flags, own_select, (((1,), (1,)), ((), ())), preferred_element_type=F32)
-    weight_ref[...] = seen[2:3] * ((peers * rows) / count[:, :1])
+    seen = lax.dot_general(
+        facts.astype(BF16), own_select, (((1,), (1,)), ((), ())), preferred_element_type=F32
+    )
+    weight_ref[...] = seen[2:3] * ((peers * rows) / count)
 
     def place(stage):
         for d in range(1, peers):
             data_copy(stage, d).wait()
         source = kv_got if stage == 0 else q_got.at[stage - 1]
-        width = source.shape[2]
-        for p in range(peers):
-            padded[p * LANES : p * LANES + room, :width] = source[p]
-        return jnp.dot(select[...], padded[:, :width], preferred_element_type=F32).astype(BF16)
-
-    lengths = [jnp.sum(one, axis=1, keepdims=True).astype(jnp.int32) for one in filled]
-    y_next = 0
-    z_next = 0
+        rows_got = source[...].reshape(peers * room, source.shape[2])
+        return jnp.dot(select[...], rows_got, preferred_element_type=F32).astype(BF16)
+
     y_count, z_count = len(y_own), len(z_jobs)
-    steps = q_stages + 1
-    for stage in range(steps):
-        while y_next < (stage + 1) * y_count // steps:
-            from_y(y_next)
-            y_next += 1
+    last = q_heads
+    for stage in range(q_heads + 1):
+        for i in range(y_count):
+            if min(i + Y_AT, last) == stage:
+                from_y(i)
+        for i in range(QUADS):
+            if min(Z_AT, last) == stage:
+                from_z(i)
         if stage == 0:
             kv_slots[...] = place(0)
             continue
-        while z_next < (stage * QUADS) // q_stages:
-            from_z(z_next)
-            z_next += 1
-        q_at = stage - 1
-        cols = slice(q_at * per_stage * DH, (q_at + 1) * per_stage * DH)
-        q_slots[:, cols] = place(stage)
-        heads = range(q_at * per_stage, (q_at + 1) * per_stage)
-        attend(q_slots, kv_slots, lengths, heads, q_heads // kv_heads, kv_heads, ctx)
-        ctx_copy(q_at).start()
+        h = stage - 1
+        q_slots[:, h * DH : (h + 1) * DH] = place(stage)
+        attend(q_slots, kv_slots, lengths, [h], q_heads // kv_heads, kv_heads, ctx)
+        ctx_copy(h).start()
     o_load.wait()
 
     def near_copy(j):
@@ -459,32 +491,33 @@
             ctx[pl.ds(mine_at, block_rows), :], ow[:, i * PIECE : (i + 1) * PIECE],
             preferred_element_type=F32,
         )
-    for stage in range(q_stages):
-        ctx_copy(stage).wait()
+    for h in range(q_heads):
+        ctx_copy(h).wait()
     for i in range(y_count):
         y_copy(i).wait_send()
 
-    def finish(i):
-        cols = slice(i * PIECE, (i + 1) * PIECE)
-        pair[:, cols] = (
-            held[:, cols] + jnp.dot(ctx_far[...], w_far[i], preferred_element_type=F32)
-        ).astype(BF16)
-        pair_copy(i).start()
-
+    def finish(which):
+        for i in which:
+            cols = slice(i * PIECE, (i + 1) * PIECE)
+            pair[:, cols] = (
+                held[:, cols] + jnp.dot(ctx_far[...], w_far[i], preferred_element_type=F32)
+            ).astype(BF16)
+        for i in which:
+            pair_copy(i).start()
+
+    x_first = 4 * QUADS
+    z_first = x_first + 2 * X_PAIRS
     for k in range(X_PAIRS):
         x_copy(2 * QUADS + k).wait()
-        finish(4 * QUADS + 2 * k)
-        finish(4 * QUADS + 2 * k + 1)
+        finish(range(x_first + 2 * k, x_first + 2 * k + 2))
     for k in range(Z_PAIRS):
         z_copy(QUADS + k).wait()
-        finish(4 * QUADS + 2 * X_PAIRS + 2 * k)
-        finish(4 * QUADS + 2 * X_PAIRS + 2 * k + 1)
+        finish(range(z_first + 2 * k, z_first + 2 * k + 2))
     for k in range(QUADS):
         z_copy(k).wait_send()
         x_copy(2 * k).wait()
         x_copy(2 * k + 1).wait()
-        for i in range(4 * k, 4 * k + 4):
-            finish(i)
+        finish(range(4 * k, 4 * k + 4))
     for n in list(range(pieces, pieces + chunks)) + list(range(pieces)):
         first, width = groups[n]
         cols = slice(first, first + width)
@@ -498,11 +531,11 @@
         mixed_ref[:, cols] = total.astype(BF16)
 
 
-def deliver(mixed_in, weight_in, mixed_hbm, weight_hbm, flat, sems):
-    big = pltpu.make_async_copy(mixed_in, mixed_hbm, sems.at[0])
+def deliver(mixed_in, weight_in, mixed_out, weight_out, flat, sems):
+    big = pltpu.make_async_copy(mixed_in, mixed_out, sems.at[0])
     big.start()
     flat[...] = weight_in[0, :]
-    small = pltpu.make_async_copy(flat, weight_hbm, sems.at[1])
+    small = pltpu.make_async_copy(flat, weight_out, sems.at[1])
     small.start()
     big.wait()
     small.wait()
@@ -520,8 +553,6 @@
     group = math.gcd(peers, 8)
     q_heads = q_weight.shape[1] // DH
     kv_heads = k_weight.shape[1] // DH
-    per_stage = math.gcd(q_heads, 2)
-    stages = q_heads // per_stage
     strips = math.gcd(rows // 16, 4)
     part = slot_count // seq_count
     out_width = o_weight.shape[1]
@@ -531,69 +562,78 @@
     chunk = math.gcd(narrow, 512)
     chunks = narrow // chunk
     kv_width = 2 * kv_heads * DH
-    q_width = per_stage * DH
     y_count = QUADS + X_PAIRS + Z_PAIRS
     x_count = 2 * QUADS + X_PAIRS
     z_count = QUADS + Z_PAIRS
     vmem = pl.BlockSpec(memory_space=pltpu.VMEM)
-    hbm = pl.BlockSpec(memory_space=pl.ANY)
+    hbm = pl.BlockSpec(memory_space=pltpu.HBM)
     dma = pltpu.SemaphoreType.DMA
     table = turn_tables()
+    buffers = [
+        pltpu.VMEM((rows, depth), BF16),
+        pltpu.VMEM((rows, 1), F32),
+        pltpu.VMEM(q_weight.shape, BF16),
+        pltpu.VMEM((depth, kv_width), BF16),
+        pltpu.VMEM(o_weight.shape, BF16),
+        pltpu.VMEM(table.shape, BF16),
+        pltpu.VMEM((peers * room, rows), BF16),
+        pltpu.VMEM((peers, 8, LANES), F32),
+        pltpu.VMEM((peers, 8, LANES), F32),
+        pltpu.VMEM((q_heads, peers, room, DH), BF16),
+        pltpu.VMEM((q_heads, peers, room, DH), BF16),
+        pltpu.VMEM((peers, room, kv_width), BF16),
+        pltpu.VMEM((peers, room, kv_width), BF16),
+        pltpu.VMEM(norm_gain.shape, F32),
+        pltpu.VMEM(q_bias.shape, F32),
+        pltpu.VMEM(k_bias.shape, F32),
+        pltpu.VMEM(v_bias.shape, F32),
+        pltpu.VMEM(positions.shape, jnp.int32),
+        pltpu.VMEM(dest_slot.shape, jnp.int32),
+        pltpu.VMEM(loss_mask.shape, jnp.int32),
+        pltpu.VMEM((slot_count, peers * room), BF16),
+        pltpu.VMEM((slot_count, q_heads * DH), BF16),
+        pltpu.VMEM((slot_count, kv_width), BF16),
+        pltpu.VMEM((slot_count, q_heads * DH), BF16),
+        pltpu.VMEM((2 * part, q_heads * DH), BF16),
+        pltpu.VMEM((pieces, o_weight.shape[0], PIECE), BF16),
+        pltpu.VMEM((2 * part, wide_cols), F32),
+        pltpu.VMEM((2 * part, out_width), BF16),
+        pltpu.VMEM((part, out_width), BF16),
+        pltpu.VMEM((2 * part, narrow), BF16),
+        pltpu.VMEM((part, narrow), BF16),
+        pltpu.VMEM((part, narrow), BF16),
+        pltpu.VMEM((part, narrow), BF16),
+        pltpu.VMEM((rows, DH), F32),
+        pltpu.VMEM((rows, DH), F32),
+        pltpu.VMEM((rows, kv_width), F32),
+    ]
+    operands = (
+        tokens, norm_gain, q_weight, k_weight, v_weight, q_bias, k_bias, v_bias, positions,
+        dest_slot, loss_mask, o_weight, jnp.asarray(table),
+    )
     mixed, weight = pl.pallas_call(
         functools.partial(
             layer_kernel, peers, group, seq_count, q_heads, kv_heads, chunk, room, strips, pieces
         ),
         in_specs=[
-            hbm, vmem, hbm, hbm, hbm, vmem, vmem, vmem, vmem, vmem, vmem, hbm, hbm,
+            hbm, hbm, hbm, hbm, hbm, hbm, hbm, hbm, hbm, hbm, hbm, hbm, hbm,
         ],
         out_specs=[vmem, vmem],
         out_shape=[
             jax.ShapeDtypeStruct((part, out_width), BF16),
             jax.ShapeDtypeStruct((1, part), F32),
         ],
-        scratch_shapes=[
-            pltpu.VMEM((rows, depth), BF16),
-            pltpu.VMEM((rows, 1), F32),
-            pltpu.VMEM(q_weight.shape, BF16),
-            pltpu.VMEM((depth, kv_width), BF16),
-            pltpu.VMEM(o_weight.shape, BF16),
-            pltpu.VMEM(table.shape, BF16),
-            pltpu.VMEM((peers * LANES, rows), BF16),
-            pltpu.VMEM((peers, 8, LANES), F32),
-            pltpu.VMEM((peers, 8, LANES), F32),
-            pltpu.VMEM((stages, peers, room, q_width), BF16),
-            pltpu.VMEM((stages, peers, room, q_width), BF16),
-            pltpu.VMEM((peers, room, kv_width), BF16),
-            pltpu.VMEM((peers, room, kv_width), BF16),
-            pltpu.VMEM((slot_count, peers * LANES), BF16),
-            pltpu.VMEM((peers * LANES, max(kv_width, q_width)), BF16),
-            pltpu.VMEM((slot_count, q_heads * DH), BF16),
-            pltpu.VMEM((slot_count, kv_width), BF16),
-            pltpu.VMEM((slot_count, q_heads * DH), BF16),
-            pltpu.VMEM((2 * part, q_heads * DH), BF16),
-            pltpu.VMEM((pieces, o_weight.shape[0], PIECE), BF16),
-            pltpu.VMEM((2 * part, wide_cols), F32),
-            pltpu.VMEM((2 * part, out_width), BF16),
-            pltpu.VMEM((part, out_width), BF16),
-            pltpu.VMEM((2 * part, narrow), BF16),
-            pltpu.VMEM((part, narrow), BF16),
-            pltpu.VMEM((part, narrow), BF16),
-            pltpu.VMEM((part, narrow), BF16),
-            pltpu.VMEM((rows, DH), F32),
-            pltpu.VMEM((rows, DH), F32),
-            dma((stages + 1, peers)), dma((stages + 1, peers)), dma((peers,)), dma((peers,)),
+        scratch_shapes=buffers + [
+            dma((q_heads + 1, peers)), dma((q_heads + 1, peers)), dma((peers,)), dma((peers,)),
             dma((chunks,)), dma((chunks,)), dma((pieces + chunks,)), dma((pieces + chunks,)),
             dma((chunks,)), dma((chunks,)), dma((strips + 5,)),
             dma((y_count,)), dma((y_count,)), dma((x_count,)), dma((x_count,)),
-            dma((z_count,)), dma((z_count,)), dma((stages,)), dma((stages,)),
+            dma((z_count,)), dma((z_count,)), dma((q_heads,)), dma((q_heads,)), dma((7,)),
         ],
         compiler_params=pltpu.CompilerParams(
             collective_id=0, has_side_effects=True, vmem_limit_bytes=VMEM_LIMIT
         ),
-    )(
-        tokens, norm_gain, q_weight, k_weight, v_weight, q_bias, k_bias, v_bias, positions,
-        dest_slot, loss_mask, o_weight, jnp.asarray(table),
-    )
+    )(*(pltpu.with_memory_space_constraint(one, pltpu.HBM) for one in operands))
     return pl.pallas_call(
         deliver,
         in_specs=[vmem, vmem],
@@ -603,6 +643,7 @@
             jax.ShapeDtypeStruct((part,), F32),
         ],
         scratch_shapes=[pltpu.VMEM((part,), F32), dma((2,))],
+        compiler_params=pltpu.CompilerParams(vmem_limit_bytes=4 * 2**20),
     )(mixed, weight)
 
 

time: 58.5 us -> 55.2 us (0.944)
  Pallas kernels: 57.5 us -> 54.3 us
    pallas_call x1, Pallas kernels: 55.1 us -> 53.2 us  [per_device(): pl.pallas_call(functools.partial(layer_kernel, peers, group, seq_count, q...]
    pallas_call x1, Pallas kernels: 2.44 us -> 1.1 us  [per_device(): pl.pallas_call(deliver, in_specs=[vmem, vmem], out_specs=[hbm, hbm], out_...]
where the time goes in v2:
time: 55.2 us; the launch traced here: 55.1 us
  Pallas kernels  54.3 us (98%)
  between operations  0.8 us (1%)
    pallas_call x1, Pallas kernels, per_device(): pl.pallas_call(functools.partial(layer_kernel, peers, group, seq_count, q...  53.2 us

profile of v2, /device:TPU:0, one launch (start us, length us, event | category | flops | bytes accessed | tf_op | source)
XLA Modules:
  0.0 55.1 jit_solution(12070362297250769442)
XLA Ops:
  0.6 53.2 %shard_map.140 = (bf16[192,3584]{1,0:T(8,128)(2,1)S(1)}, f32[1,192]{1,0:T(1,128)S(1)}) custom-call(bf16[576,3584]{1,0:T(8,128)(2,1)} %tok_hbm.1, f32[3584]{0:T(1024)} %gain_hbm.1, bf16[3584,512]{1,0:T(8,128)(2,1)} %qw_hbm.1, bf16[3584,128]{1,0:T(8,128)(2,1)} %kw_hbm.1, bf16[3584,128]{1,0:T(8,128)(2,1)} %vw_hbm.1, f32[512]{0:T(512)} %qb_hbm.1, f32[128]{0:T(128)} %kb_hbm.1, ...), custom_call_target="tpu_custom_call" | custom-call | tf_op jit(solution)/shard_map/pallas_call | solution.py:614
  53.8 1.1 %shard_map.141 = (bf16[192,3584]{1,0:T(8,128)(2,1)}, f32[192]{0:T(256)}) custom-call(bf16[192,3584]{1,0:T(8,128)(2,1)S(1)} %get-tuple-element.4.mixed_in, f32[1,192]{1,0:T(1,128)S(1)} %get-tuple-element.5.weight_in), custom_call_target="tpu_custom_call" | custom-call | tf_op jit(solution)/shard_map/pallas_call | solution.py:637

commit v3 on v2

--- a/solution.py
+++ b/solution.py
@@ -13,8 +13,8 @@
 BUCKET = 384
 LANES = 128
 PIECE = 256
-QUADS, X_PAIRS, Z_PAIRS = 1, 2, 1
-Y_AT, Z_AT = 0, 3
+QUADS, X_PAIRS, Z_PAIRS = 1, 2, 2
+Y_AT, Z_AT = 0, 4
 VMEM_LIMIT = 52000000
 
 NORM_EPSILON = 1e-06
@@ -340,6 +340,12 @@
     for i in range(strips // 2):
         token_loads[i].wait()
         norm(i)
+    pl.semaphore_wait(barrier, peers + 1)
+    for i in range(len(y_own)):
+        y_copy(i).start()
+    for d in range(1, peers):
+        info_copy(d).start()
+    got_info[me] = told_out[me]
     for i in range(strips // 2, strips):
         token_loads[i].wait()
     k_load.wait()
@@ -360,13 +366,7 @@
             head = turn(head.astype(F32)).astype(BF16)
         heads_out.append(head)
     pack(jnp.concatenate(heads_out, axis=1), [kv_out])
-    pl.semaphore_wait(barrier, peers + 1)
     send(0)
-    for i in range(len(y_own)):
-        y_copy(i).start()
-    for d in range(1, peers):
-        info_copy(d).start()
-    got_info[me] = told_out[me]
     q_load.wait()
     o_load.start()
     for first in range(0, q_heads, together):

time: 55.2 us -> 53.2 us (0.964)
  Pallas kernels: 54.3 us -> 52.2 us
    pallas_call x1, Pallas kernels: 53.2 us -> 51.1 us  [per_device(): pl.pallas_call(functools.partial(layer_kernel, peers, group, seq_count, q...]
where the time goes in v3:
time: 53.2 us; the launch traced here: 53 us
  Pallas kernels  52.2 us (98%)
  between operations  0.8 us (2%)
    pallas_call x1, Pallas kernels, per_device(): pl.pallas_call(functools.partial(layer_kernel, peers, group, seq_count, q...  51.1 us
    pallas_call x1, Pallas kernels, per_device(): pl.pallas_call(deliver, in_specs=[vmem, vmem], out_specs=[hbm, hbm], out_...  1.1 us

profile of v3, /device:TPU:0, one launch (start us, length us, event | category | flops | bytes accessed | tf_op | source)
XLA Modules:
  0.0 53.0 jit_solution(12020481279741852808)
XLA Ops:
  0.6 51.1 %shard_map.140 = (bf16[192,3584]{1,0:T(8,128)(2,1)S(1)}, f32[1,192]{1,0:T(1,128)S(1)}) custom-call(bf16[576,3584]{1,0:T(8,128)(2,1)} %tok_hbm.1, f32[3584]{0:T(1024)} %gain_hbm.1, bf16[3584,512]{1,0:T(8,128)(2,1)} %qw_hbm.1, bf16[3584,128]{1,0:T(8,128)(2,1)} %kw_hbm.1, bf16[3584,128]{1,0:T(8,128)(2,1)} %vw_hbm.1, f32[512]{0:T(512)} %qb_hbm.1, f32[128]{0:T(128)} %kb_hbm.1, ...), custom_call_target="tpu_custom_call" | custom-call | tf_op jit(solution)/shard_map/pallas_call | solution.py:614
  51.7 1.1 %shard_map.141 = (bf16[192,3584]{1,0:T(8,128)(2,1)}, f32[192]{0:T(256)}) custom-call(bf16[192,3584]{1,0:T(8,128)(2,1)S(1)} %get-tuple-element.4.mixed_in, f32[1,192]{1,0:T(1,128)S(1)} %get-tuple-element.5.weight_in), custom_call_target="tpu_custom_call" | custom-call | tf_op jit(solution)/shard_map/pallas_call | solution.py:637
